TPU v7x, 256 devices: a whole 4x4x8 slice. The times are simulated.
256 devices in a mesh: gx: 8 (over y, core), gy: 4 (over x), gz: 8 (over z).
Axes of the slice: x: 4, y: 4, z: 8, core: 2. Of those that a mesh axis runs over, the one named last changes fastest.
Arguments:
- leaf_coeffs: float32 [4096, 1000], P(('gx', 'gy', 'gz')), may hold values from -6 to 6
- operator_blocks: float32 [2, 7, 4, 3, 400], replicated, may hold values from -0.5 to 0.5
- term_ranks: int32 [2, 7], replicated, may hold values from 2 to 4
- target_device: int32 [512, 7, 1], P(('gx', 'gy', 'gz')), may hold values from 0 to 31; in each aligned block of 14 rows (0 to 13, 14 to 27, ..., all dimensions but the last counted through in order) at most 2 rows name the same one
- target_slot: int32 [512, 7], P(('gx', 'gy', 'gz')), may hold values from 0 to 1
- coarse_targets: int32 [96, 7], P(('gx', 'gy')), may hold values from 0 to 95
- parent_place: int32 [32, 16], P(('gx', 'gy')), may hold values from 0 to 23, as said below
Outputs:
- leaf_result: float32 [4096, 1000], P(('gx', 'gy', 'gz'))
Inputs may be any that keep to these rules, and one draw needn't show every extreme that they name: `parent_place`: each row names distinct values. `target_device`: among the rows of one device, no value is named more than 2 times.
All inputs are finite; a program needn't handle non-finite values.
Results may differ from a plain program's by a relative error of at most 0.0003.
Values sent between devices are 32-bit elements; how exact they have to be, the bound alone decides.
No kernel may reach another device: no remote copies, remote signals or barrier semaphores. Data moves between devices by JAX's collectives and lax.ppermute only.
A program may use at most 64 MiB of HBM per device.

v0:
```python
import jax
import jax.numpy as jnp
import numpy as np
from jax import lax
from jax.experimental import pallas as pl
from jax.experimental.pallas import tpu as pltpu
from jax.sharding import PartitionSpec as P

ORDER = 10
EDGE = 20
ZPAD = 24
LANES = 512
DISP = 7
TERMS = 4
SLOTS = 8
C0 = 3
NODES1 = 2
F32 = jnp.float32
BF16 = jnp.bfloat16


def _tables():
    n = EDGE
    i = np.arange(n)[:, None]
    x = np.arange(n)[None, :]
    h = np.sqrt(2.0 / n) * np.cos(np.pi * (x + 0.5) * i / n)
    h[0] *= np.sqrt(0.5)
    c = {}
    perm = np.zeros((LANES, LANES))
    for oy in range(2):
        for oz in range(2):
            for b in range(10):
                for k in range(10):
                    perm[(2 * oy + oz) * 128 + 10 * b + k, (10 * oy + b) * ZPAD + 10 * oz + k] = 1
    c["perm"] = perm
    c["permt"] = perm.T.copy()
    ra = np.zeros((4, 40, 160))
    rt = np.zeros((160, 160))
    for nn in range(2):
        for ox in range(2):
            for oyz in range(4):
                for a in range(10):
                    row = nn * 20 + ox * 10 + a
                    leaf = 8 * nn + 4 * ox + oyz
                    ra[oyz, row, a * 16 + leaf] = 1
                    rt[a * 16 + leaf, oyz * 40 + row] = 1
    c["ra"] = ra
    c["rt"] = rt
    hx = np.zeros((24, 40))
    ht = np.zeros((40, 24))
    for nn in range(2):
        for ii in range(10):
            for xx in range(20):
                hx[ii * 2 + nn, nn * 20 + xx] = h[ii, xx]
                ht[nn * 20 + xx, nn * 12 + ii] = h[ii, xx]
    c["hx"] = hx
    c["ht"] = ht
    hy = np.zeros((LANES, 128))
    for y in range(20):
        for z in range(20):
            hy[y * ZPAD + z, :100] = np.outer(h[:10, y], h[:10, z]).reshape(-1)
    c["hy"] = hy
    c["hyt"] = hy.T.copy()
    ca = np.zeros((24, 400))
    ci = np.zeros((24, 400))
    g0 = np.zeros((400, 160))
    g1 = np.zeros((400, LANES))
    g2 = np.zeros((400, LANES))
    for ii in range(20):
        for a in range(20):
            q = ii * 20 + a
            ca[:20, q] = h[a]
            ci[:20, q] = h[ii]
            g0[q] = np.repeat(h[a], SLOTS)
            for y in range(20):
                g1[q, y * ZPAD : y * ZPAD + 20] = h[ii, y]
                g2[q, y * ZPAD : y * ZPAD + 20] = h[ii]
    c["ca"], c["ci"], c["g0"], c["g1"], c["g2"] = ca, ci, g0, g1, g2
    po = np.zeros((160, 160))
    for xx in range(20):
        for r in range(8):
            po[(r // 2) * 40 + (r % 2) * 20 + xx, xx * 8 + r] = 1
    c["po"] = po
    out = {k: np.asarray(v, np.float32) for k, v in c.items()}
    return out


def _onehot(t):
    return jnp.asarray(t, BF16)


def _pair(t):
    t = np.asarray(t, np.float32)
    hi = t.astype(jnp.bfloat16)
    lo = (t - hi.astype(np.float32)).astype(jnp.bfloat16)
    return jnp.asarray(np.stack([hi, lo]))


def dot(a, b):
    return jnp.dot(a, b, preferred_element_type=F32)


def dot_nt(a, b):
    return lax.dot_general(a, b, (((1,), (1,)), ((), ())), preferred_element_type=F32)


def split2(v):
    hi = v.astype(BF16)
    return hi, (v - hi.astype(F32)).astype(BF16)


def split3(v):
    hi = v.astype(BF16)
    rest = v - hi.astype(F32)
    mid = rest.astype(BF16)
    return hi, mid, (rest - mid.astype(F32)).astype(BF16)


def dot3(a, b):
    ah, al = a
    bh, bl = b
    return dot(ah, bh) + (dot(al, bh) + dot(ah, bl))


def iota(shape, dim):
    return lax.broadcasted_iota(jnp.int32, shape, dim)


def pack_kernel(leaf, td, ts, ct, pp, ra, perm, hx, hy, wmsg, cmsg, rows):
    rows[...] = jnp.zeros_like(rows)
    for a in range(ORDER):
        rows[16 * a : 16 * a + 16, :100] = leaf[:, 100 * a : 100 * a + 100]
    w = jnp.zeros((40, LANES), F32)
    for part in split3(rows[...]):
        pieces = [dot(ra[o], part) for o in range(4)]
        w = w + dot(jnp.concatenate(pieces, axis=1).astype(BF16), perm[...])
    first = dot3((hx[0], hx[1]), split2(w))
    corner = dot3(split2(first), (hy[0], hy[1]))
    lane = iota((40, LANES), 1)
    row = iota((40, LANES), 0)
    for n in range(NODES1):
        mine = (row // EDGE) == n
        for e in range(DISP):
            w = jnp.where(mine & (lane == 480 + e), td[n, e].astype(F32), w)
            w = jnp.where(mine & (lane == 488 + e), ts[n, e].astype(F32), w)
    wmsg[...] = w
    z = lax.axis_index("gz")
    lane2 = iota((2, 128), 1)
    row2 = iota((2, 128), 0)
    head = corner[0:2, :]
    for n in range(NODES1):
        q = pp[0, z * NODES1 + n]
        head = jnp.where((row2 == n) & (lane2 == 108), (q % 8).astype(F32), head)
        for e in range(DISP):
            head = jnp.where((row2 == n) & (lane2 == 100 + e), ct[q // 8, e].astype(F32), head)
    cmsg[:, 0:128] = head
    for i in range(1, ORDER):
        cmsg[:, 128 * i : 128 * i + 128] = corner[2 * i : 2 * i + 2, :]


def prep_kernel(ob, ranks, ci, ca, g0, g1, g2, a0, l1, l2, q0, q1, q2):
    level = pl.program_id(0)
    for e in range(DISP):
        for t in range(TERMS):
            k = e * TERMS + t
            keep = (t < ranks[level, e]).astype(F32)
            q0[24 * k : 24 * k + 24, :] = ob[0, e, t, 0:1, :] * keep * ci[...]
            q1[24 * k : 24 * k + 24, :] = ob[0, e, t, 1:2, :] * ca[...]
            q2[24 * k : 24 * k + 24, :] = ob[0, e, t, 2:3, :] * ca[...]
    a0[0] = dot3(split2(q0[...]), (g0[0], g0[1]))
    l1[0] = dot3(split2(q1[...]), (g1[0], g1[1]))
    l2[0] = dot3(split2(q2[...]), (g2[0], g2[1]))


def images(source, a0, l1, l2, acc, kh, kl, bd):
    first = pl.program_id(0) == 0

    @pl.when(first)
    def _():
        acc[...] = jnp.zeros_like(acc)
        for t in range(TERMS):
            kh[t, 480:, :] = jnp.zeros((32, LANES), BF16)
            kl[t, 480:, :] = jnp.zeros((32, LANES), BF16)

    src = split2(source)
    same = ((iota((8, 160), 1) % 8) == iota((8, 160), 0)).astype(F32)
    total = acc[...]
    for t in range(TERMS):
        for i in range(EDGE):
            bd[t, 8 * i : 8 * i + 8, :] = a0[0, 24 * t + i : 24 * t + i + 1, :] * same
        third = l2[0, 24 * t : 24 * t + 24, :]
        for y in range(0, EDGE, 2):
            one = l1[0, 24 * t + y : 24 * t + y + 1, :] * third
            two = l1[0, 24 * t + y + 1 : 24 * t + y + 2, :] * third
            hi, lo = split2(jnp.concatenate([one, two], axis=0))
            kh[t, ZPAD * y : ZPAD * y + 48, :] = hi
            kl[t, ZPAD * y : ZPAD * y + 48, :] = lo
        mixed = split2(dot3(split2(bd[t]), src))
        total = total + dot3(mixed, (kh[t], kl[t]))
    acc[...] = total


def coarse_kernel(corners, pp, a0, l1, l2, perm, permt, out, acc, kh, kl, bd, gs, sw):
    e = pl.program_id(0)

    @pl.when(e == 0)
    def _():
        sel = (iota((16, 128), 1) == iota((16, 128), 0) + 100).astype(BF16)
        info = dot_nt(sel, corners[:, 0:128].astype(BF16))
        col = lax.axis_index("gx") * lax.axis_size("gy") + lax.axis_index("gy")
        r8 = iota((8, 64), 0)
        want = jnp.where(r8 < C0, (col * C0 + r8), -1).astype(F32)
        octant = info[8:9, :]
        blocks = []
        for oyz in range(4):
            for d in range(DISP):
                hit = info[d : d + 1, :] == want
                for ox in range(2):
                    there = octant == float(4 * ox + oyz)
                    blocks.append(jnp.where(hit & there, 1.0, 0.0))
        pick = jnp.concatenate(blocks, axis=0).astype(BF16)
        hi, lo = split2(corners[...])
        gs[...] = dot(pick, hi) + dot(pick, lo)

    for oyz in range(4):
        for ox in range(2):
            base = (oyz * DISP + e) * 16 + ox * 8
            for a in range(ORDER):
                sw[(ox * 10 + a) * 8 : (ox * 10 + a) * 8 + 8, 128 * oyz : 128 * oyz + 128] = gs[
                    pl.ds(base, 8), 128 * a : 128 * a + 128
                ]
    hi, lo = split2(sw[...])
    source = dot(hi, perm[...]) + dot(lo, perm[...])
    images(source, a0, l1, l2, acc, kh, kl, bd)

    @pl.when(e == DISP - 1)
    def _():
        col = iota((ZPAD, 640), 1)
        code = ((col % 8) * 4 + col // 160) * EDGE + (col % 160) // 8
        row = iota((ZPAD, 640), 0)
        a = row % 12
        blocks = []
        for z in range(8):
            qs = [pp[0, NODES1 * z + n] for n in range(NODES1)]
            bases = [((q // 8) * 4 + q % 4) * EDGE + ((q % 8) // 4) * ORDER for q in qs]
            base = jnp.where(row < 12, bases[0], bases[1])
            blocks.append(jnp.where((a < ORDER) & (code == base + a), 1.0, 0.0))
        pick = jnp.concatenate(blocks, axis=0).astype(BF16)
        picked = jnp.zeros((192, 128), F32)
        for part in split3(acc[...]):
            moved = dot(part, permt[...]).astype(BF16)
            stacked = jnp.concatenate([moved[:, 128 * o : 128 * o + 128] for o in range(4)], axis=0)
            picked = picked + dot(pick, stacked)
        for z in range(8):
            out[z] = picked[ZPAD * z : ZPAD * z + ZPAD, :]


def middle_kernel(wall, a0, l1, l2, po, out, acc, kh, kl, bd, info):
    e = pl.program_id(0)

    @pl.when(e == 0)
    def _():
        sel = (iota((16, 128), 1) == iota((16, 128), 0) + 96).astype(BF16)
        raw = dot_nt(sel, wall[:, 384:512].astype(BF16))
        device = raw[0:8, :]
        gy = jnp.floor(device * 0.125)
        gz = device - gy * 8.0
        z = lax.axis_index("gz").astype(F32)
        info[...] = jnp.where(gz == z, gy * 2.0 + raw[8:16, :], -1.0)

    lane = iota((160, 320), 1)
    row = iota((160, 320), 0)
    target = info[pl.ds(e, 1), :]
    hit = (lane % EDGE == row // 8) & (target == (row % 8).astype(F32))
    pick = jnp.where(hit, 1.0, 0.0).astype(BF16)
    hi, lo = split2(wall[...])
    source = dot(pick, hi) + dot(pick, lo)
    images(source, a0, l1, l2, acc, kh, kl, bd)

    @pl.when(e == DISP - 1)
    def _():
        moved = jnp.zeros((160, LANES), F32)
        for part in split3(acc[...]):
            moved = moved + dot(po[...], part)
        for g in range(4):
            out[g] = moved[40 * g : 40 * g + 40, :]


def final_kernel(mid, coarse, ht, hyt, permt, rt, out):
    total = (mid[0] + mid[1]) + (mid[2] + mid[3])
    corner = coarse[0]
    for z in range(1, 8):
        corner = corner + coarse[z]
    up = dot3((ht[0], ht[1]), split2(corner))
    total = total + dot3(split2(up), (hyt[0], hyt[1]))
    rows = jnp.zeros((160, 128), F32)
    for part in split3(total):
        moved = dot(part, permt[...]).astype(BF16)
        stacked = jnp.concatenate([moved[:, 128 * o : 128 * o + 128] for o in range(4)], axis=0)
        rows = rows + dot(rt[...], stacked)
    for a in range(ORDER):
        out[:, 100 * a : 100 * a + 100] = rows[16 * a : 16 * a + 16, :100]


VM = pl.BlockSpec(memory_space=pltpu.MemorySpace.VMEM)
SM = pl.BlockSpec(memory_space=pltpu.MemorySpace.SMEM)
INTERPRET = False


def sds(*shape):
    return jax.ShapeDtypeStruct(shape, F32)


def _params():
    return pltpu.CompilerParams(vmem_limit_bytes=56 * 1024 * 1024)


def level_specs():
    def of(rows, lanes):
        return pl.BlockSpec((1, rows, lanes), lambda e: (0, e, 0))

    return [of(96, 160), of(96, LANES), of(96, LANES)]


def level_scratch():
    return [
        pltpu.VMEM((160, LANES), F32),
        pltpu.VMEM((TERMS, LANES, LANES), BF16),
        pltpu.VMEM((TERMS, LANES, LANES), BF16),
        pltpu.VMEM((TERMS, 160, 160), F32),
    ]


def const(shape):
    return pl.BlockSpec(shape, lambda *_: (0,) * len(shape))


def gather_rows(value, axis):
    copies = jnp.broadcast_to(value, (lax.axis_size(axis), *value.shape))
    return lax.all_to_all(copies, axis, split_axis=0, concat_axis=0, tiled=True)


def on_device(leaf, ob, ranks, td, ts, ct, pp):
    c = _tables()
    perm, permt = _onehot(c["perm"]), _onehot(c["permt"])
    wmsg, cmsg = pl.pallas_call(
        pack_kernel,
        out_shape=(sds(40, LANES), sds(2, 1280)),
        in_specs=[VM, SM, SM, SM, SM, VM, VM, VM, VM],
        out_specs=(VM, VM),
        scratch_shapes=[pltpu.VMEM((160, 128), F32)],
        compiler_params=_params(),
        interpret=INTERPRET,
        name="pack",
    )(
        leaf,
        td.reshape(NODES1, DISP),
        ts,
        ct,
        pp,
        _onehot(c["ra"]),
        perm,
        _pair(c["hx"]),
        _pair(c["hy"]),
    )
    corners = gather_rows(cmsg, ("gx", "gy")).reshape(64, 1280)
    wall = gather_rows(wmsg, "gz").reshape(320, LANES)
    rows = DISP * TERMS * 24
    mats = pl.pallas_call(
        prep_kernel,
        grid=(2,),
        out_shape=(sds(2, rows, 160), sds(2, rows, LANES), sds(2, rows, LANES)),
        in_specs=[
            pl.BlockSpec((1, DISP, TERMS, 3, 400), lambda l: (l, 0, 0, 0, 0)),
            SM,
            const((24, 400)),
            const((24, 400)),
            const((2, 400, 160)),
            const((2, 400, LANES)),
            const((2, 400, LANES)),
        ],
        out_specs=tuple(
            pl.BlockSpec((1, rows, n), lambda l: (l, 0, 0)) for n in (160, LANES, LANES)
        ),
        scratch_shapes=[pltpu.VMEM((rows, 400), F32)] * 3,
        compiler_params=_params(),
        interpret=INTERPRET,
        name="prep",
    )(
        ob,
        ranks,
        jnp.asarray(c["ci"]),
        jnp.asarray(c["ca"]),
        _pair(c["g0"]),
        _pair(c["g1"]),
        _pair(c["g2"]),
    )

    def specs(level):
        def of(lanes):
            return pl.BlockSpec((1, 96, lanes), lambda e: (level, e, 0))

        return [of(160), of(LANES), of(LANES)]

    coarse = pl.pallas_call(
        coarse_kernel,
        grid=(DISP,),
        out_shape=sds(8, 24, 128),
        in_specs=[
            const((64, 1280)),
            SM,
            *specs(0),
            const((LANES, LANES)),
            const((LANES, LANES)),
        ],
        out_specs=const((8, 24, 128)),
        scratch_shapes=[
            *level_scratch(),
            pltpu.VMEM((448, 1280), F32),
            pltpu.VMEM((160, LANES), F32),
        ],
        compiler_params=_params(),
        interpret=INTERPRET,
        name="coarse",
    )(corners, pp, *mats, perm, permt)
    middle = pl.pallas_call(
        middle_kernel,
        grid=(DISP,),
        out_shape=sds(4, 40, LANES),
        in_specs=[const((320, LANES)), *specs(1), const((160, 160))],
        out_specs=const((4, 40, LANES)),
        scratch_shapes=[*level_scratch(), pltpu.VMEM((8, 320), F32)],
        compiler_params=_params(),
        interpret=INTERPRET,
        name="middle",
    )(wall, *mats, _onehot(c["po"]))
    coarse = lax.all_to_all(coarse, "gz", split_axis=0, concat_axis=0, tiled=True)
    middle = lax.all_to_all(middle, "gy", split_axis=0, concat_axis=0, tiled=True)
    return pl.pallas_call(
        final_kernel,
        out_shape=sds(16, 1000),
        in_specs=[VM] * 6,
        out_specs=VM,
        compiler_params=_params(),
        interpret=INTERPRET,
        name="final",
    )(middle, coarse, _pair(c["ht"]), _pair(c["hyt"]), permt, _onehot(c["rt"]))


def solution(mesh):
    in_specs = (
        P(("gx", "gy", "gz"), None),
        P(),
        P(),
        P(("gx", "gy", "gz"), None, None),
        P(("gx", "gy", "gz"), None),
        P(("gx", "gy"), None),
        P(("gx", "gy"), None),
    )
    out_specs = P(("gx", "gy", "gz"), None)
    return jax.shard_map(
        on_device, mesh=mesh, in_specs=in_specs, out_specs=out_specs, check_vma=False
    )
```

profile of v0, /device:TPU:32, one launch (start us, length us, event | category | flops | bytes accessed | tf_op | source)
XLA Modules:
  0.0 105.1 jit_solution(9944774382977752777)
XLA Ops:
  0.0 0.0 copy-start.2
  0.0 3.0 %pack.1 = (f32[40,512]{1,0:T(8,128)}, f32[2,1280]{1,0:T(2,128)}) custom-call(f32[16,1000]{1,0:T(8,128)} %leaf.1, s32[2,7]{1,0:T(2,128)} %bitcast.3, s32[2,7]{1,0:T(2,128)} %ts.1, s32[3,7]{1,0:T(4,128)} %ct.1, s32[1,16]{1,0:T(1,128)} %pp.3, bf16[4,40,160]{2,1,0:T(8,128)(2,1)} %constant.30.clone.ra, bf16[512,512]{1,0:T(8,128)(2,1)} %constant.28.clone.perm, ...), custom_call_target="tpu_custom_call" | custom-call | tf_op jit(solution)/shard_map/pack/pallas_call | solution.py:346
  3.0 0.8 broadcast_in_dim.7
  3.8 16.7 %all_to_all.20 = f32[32,2,1280]{2,1,0:T(2,128)S(1)} all-to-all(f32[32,2,1280]{2,1,0:T(2,128)S(1)} %broadcast_in_dim.7), channel_id=1, replica_groups=mesh['gx'=8,'gy'=4,'gz'=8] {'gx','gy'}, dimensions={0} | all-to-all | bytes 655360 | tf_op jit(solution)/shard_map/all_to_all | solution.py:340
  20.5 1.8 %broadcast_in_dim.6 = f32[8,40,512]{2,1,0:T(8,128)} broadcast(f32[40,512]{1,0:T(8,128)} %get-tuple-element.10), dimensions={1,2} | broadcast | bytes 737280 | tf_op jit(solution)/shard_map/broadcast_in_dim | solution.py:339
  22.3 8.6 %all-to-all-start = ((f32[8,40,512]{2,1,0:T(8,128)}), f32[8,40,512]{2,1,0:T(8,128)S(1)}, u32[]{:S(2)}, u32[]{:S(2)}) async-start(f32[8,40,512]{2,1,0:T(8,128)} %broadcast_in_dim.6), calls=%async_computation | async-start | bytes 1310720 | tf_op jit(solution)/shard_map/all_to_all | solution.py:340
  30.9 0.0 copy-done.2
  30.9 1.0 copy.22.ob
  31.8 9.1 %prep.1 = (f32[2,672,160]{2,1,0:T(8,128)}, f32[2,672,512]{2,1,0:T(8,128)}, f32[2,672,512]{2,1,0:T(8,128)}) custom-call(f32[2,7,4,3,400]{4,3,2,1,0:T(4,128)} %copy.22.ob, s32[2,7]{1,0:T(2,128)} %ranks.1, f32[24,400]{1,0:T(8,128)} %constant.33.clone.ci, f32[24,400]{1,0:T(8,128)} %constant.34.clone.ca, bf16[2,400,160]{2,1,0:T(8,128)(2,1)} %constant.35.clone.g0, ...), custom_call_target="tpu_custom_call" | custom-call | tf_op jit(solution)/shard_map/prep/pallas_call | solution.py:369
  40.9 0.9 reshape.11.corners
  41.8 21.6 %coarse.1 = f32[8,24,128]{2,1,0:T(8,128)} custom-call(f32[64,1280]{1,0:T(8,128)} %reshape.11.corners, s32[1,16]{1,0:T(1,128)} %pp.3, f32[2,672,160]{2,1,0:T(8,128)} %get-tuple-element.11.a0, f32[2,672,512]{2,1,0:T(8,128)} %get-tuple-element.12.l1, f32[2,672,512]{2,1,0:T(8,128)} %get-tuple-element.13.l2, bf16[512,512]{1,0:T(8,128)(2,1)} %constant.28.clone.perm, ...), custom_call_target="tpu_custom_call" | custom-call | tf_op jit(solution)/shard_map/coarse/pallas_call | solution.py:405
  63.4 0.0 all-to-all-done
  63.4 0.0 copy-start
  63.4 7.2 %all-to-all-start.3 = ((f32[8,24,128]{2,1,0:T(8,128)}), f32[8,24,128]{2,1,0:T(8,128)S(1)}, u32[]{:S(2)}, u32[]{:S(2)}) async-start(f32[8,24,128]{2,1,0:T(8,128)} %coarse.1), calls=%async_computation.3 | async-start | bytes 196608 | tf_op jit(solution)/shard_map/all_to_all | solution.py:437
  70.7 0.0 copy-done
  70.7 20.2 %middle.1 = f32[4,40,512]{2,1,0:T(8,128)} custom-call(f32[320,512]{1,0:T(8,128)} %bitcast.2, f32[2,672,160]{2,1,0:T(8,128)} %get-tuple-element.11.a0, f32[2,672,512]{2,1,0:T(8,128)} %get-tuple-element.12.l1, f32[2,672,512]{2,1,0:T(8,128)} %get-tuple-element.13.l2, bf16[160,160]{1,0:T(8,128)(2,1)} %constant.38.clone.po), custom_call_target="tpu_custom_call" | custom-call | tf_op jit(solution)/shard_map/middle/pallas_call | solution.py:426
  90.9 0.0 all-to-all-done.3.coarse
  90.9 0.0 copy-start.1
  90.9 11.2 %all_to_all.21.mid = f32[4,40,512]{2,1,0:T(8,128)} all-to-all(f32[4,40,512]{2,1,0:T(8,128)} %middle.1), channel_id=1, replica_groups=mesh['gx'=8,'gy'=4,'gz'=8] {'gy'}, dimensions={0} | all-to-all | bytes 655360 | tf_op jit(solution)/shard_map/all_to_all | solution.py:438
  102.1 0.0 copy-done.1
  102.1 3.0 %final.1 = f32[16,1000]{1,0:T(8,128)} custom-call(f32[4,40,512]{2,1,0:T(8,128)} %all_to_all.21.mid, f32[8,24,128]{2,1,0:T(8,128)} %copy-done.1, bf16[2,40,24]{2,1,0:T(8,128)(2,1)} %constant.39.clone.ht, bf16[2,128,512]{2,1,0:T(8,128)(2,1)} %constant.40.clone.hyt, bf16[512,512]{1,0:T(8,128)(2,1)} %constant.29.clone.permt, bf16[160,160]{1,0:T(8,128)(2,1)} %constant.41.clone.rt), custom_call_target="tpu_custom_call" | custom-call | tf_op jit(solution)/shard_map/final/pallas_call | solution.py:439
Async XLA Ops:
  0.0 30.9 %copy-start.2 = (f32[2,7,4,3,400]{4,2,3,1,0:T(4,128)S(1)}, f32[2,7,4,3,400]{4,2,3,1,0:T(4,128)}, u32[]{:S(2)}) copy-start(f32[2,7,4,3,400]{4,2,3,1,0:T(4,128)} %param.22) | copy-start | bytes 806404
  22.3 41.1 %all-to-all-start = ((f32[8,40,512]{2,1,0:T(8,128)}), f32[8,40,512]{2,1,0:T(8,128)S(1)}, u32[]{:S(2)}, u32[]{:S(2)}) async-start(f32[8,40,512]{2,1,0:T(8,128)} %broadcast_in_dim.6), calls=%async_computation | async-start | bytes 1310720 | tf_op jit(solution)/shard_map/all_to_all | solution.py:340
  63.4 7.2 %copy-start = (f32[8,40,512]{2,1,0:T(8,128)}, f32[8,40,512]{2,1,0:T(8,128)S(1)}, u32[]{:S(2)}) copy-start(f32[8,40,512]{2,1,0:T(8,128)S(1)} %all-to-all-done) | copy-start | bytes 1966084
  63.4 27.4 %all-to-all-start.3 = ((f32[8,24,128]{2,1,0:T(8,128)}), f32[8,24,128]{2,1,0:T(8,128)S(1)}, u32[]{:S(2)}, u32[]{:S(2)}) async-start(f32[8,24,128]{2,1,0:T(8,128)} %coarse.1), calls=%async_computation.3 | async-start | bytes 196608 | tf_op jit(solution)/shard_map/all_to_all | solution.py:437
  90.9 11.2 %copy-start.1 = (f32[8,24,128]{2,1,0:T(8,128)}, f32[8,24,128]{2,1,0:T(8,128)S(1)}, u32[]{:S(2)}) copy-start(f32[8,24,128]{2,1,0:T(8,128)S(1)} %all-to-all-done.3.coarse) | copy-start | bytes 294916
where the time goes:
time: 106 us; the launch traced here: 105 us
  Pallas kernels  56.9 us (54%)
  blocking collectives  27.9 us (26%)
  starting transfers between devices  15.8 us (15%)
  local copies, waits for them, and re-layouts  4.5 us (4%)
    pallas_call x1, Pallas kernels, on_device(): pl.pallas_call(coarse_kernel, grid=(DISP,), out_shape=sds(8, 24, 128), in...  21.6 us
    pallas_call x1, Pallas kernels, on_device(): pl.pallas_call(middle_kernel, grid=(DISP,), out_shape=sds(4, 40, LANES),...  20.2 us
    all_to_all x1, blocking collectives, gather_rows(): return lax.all_to_all(copies, axis, split_axis=0, concat_axis=0, tiled=True)  16.7 us
    all_to_all x1, blocking collectives, on_device(): lax.all_to_all(middle, 'gy', split_axis=0, concat_axis=0, tiled=True)  11.2 us
    pallas_call x1, Pallas kernels, on_device(): pl.pallas_call(prep_kernel, grid=(2,), out_shape=(sds(2, rows, 160), sds(...  9.07 us
    all_to_all x1, starting transfers between devices, gather_rows(): return lax.all_to_all(copies, axis, split_axis=0, concat_axis=0, tiled=True)  8.57 us
    all_to_all x1, starting transfers between devices, on_device(): lax.all_to_all(coarse, 'gz', split_axis=0, concat_axis=0, tiled=True)  7.23 us
    pallas_call x1, Pallas kernels, on_device(): pl.pallas_call(final_kernel, out_shape=sds(16, 1000), in_specs=[VM] * 6,...  3.03 us
  transfers between devices with their start and end apart: 2, of which 0 were waited for; matrix products, arithmetic and copies ran while one was open for 2% of the time, Pallas kernels for 48%

commit v1 on v0

v1 whole, which is shorter than its diff:
```python
import jax
import jax.numpy as jnp
import numpy as np
from jax import lax
from jax.experimental import pallas as pl
from jax.experimental.pallas import tpu as pltpu
from jax.sharding import PartitionSpec as P

ORDER = 10
EDGE = 20
ZPAD = 24
LANES = 512
DISP = 7
TERMS = 4
SLOTS = 8
C0 = 3
NODES1 = 2
F32 = jnp.float32
BF16 = jnp.bfloat16


def _tables():
    n = EDGE
    i = np.arange(n)[:, None]
    x = np.arange(n)[None, :]
    h = np.sqrt(2.0 / n) * np.cos(np.pi * (x + 0.5) * i / n)
    h[0] *= np.sqrt(0.5)
    c = {}
    lanes = np.full((8, LANES), -1)
    for y in range(EDGE):
        for z in range(EDGE):
            at = (2 * (y // 10) + z // 10) * 128 + (y % 10) * 10 + z % 10
            lanes[0, y * ZPAD + z] = at
            lanes[1, at] = y * ZPAD + z
    c["lanes"] = lanes
    ra = np.zeros((4, 40, 160))
    rt = np.zeros((160, 160))
    for nn in range(2):
        for ox in range(2):
            for oyz in range(4):
                for a in range(10):
                    row = nn * 20 + ox * 10 + a
                    leaf = 8 * nn + 4 * ox + oyz
                    ra[oyz, row, a * 16 + leaf] = 1
                    rt[a * 16 + leaf, oyz * 40 + row] = 1
    c["ra"] = ra
    c["rt"] = rt
    hx = np.zeros((24, 40))
    ht = np.zeros((40, 24))
    for nn in range(2):
        for ii in range(10):
            for xx in range(20):
                hx[ii * 2 + nn, nn * 20 + xx] = h[ii, xx]
                ht[nn * 20 + xx, nn * 12 + ii] = h[ii, xx]
    c["hx"] = hx
    c["ht"] = ht
    hy = np.zeros((LANES, 128))
    for y in range(20):
        for z in range(20):
            hy[y * ZPAD + z, :100] = np.outer(h[:10, y], h[:10, z]).reshape(-1)
    c["hy"] = hy
    c["hyt"] = hy.T.copy()
    ca = np.zeros((24, 400))
    ci = np.zeros((24, 400))
    folds = np.zeros((2, 400, 128))
    wide = np.zeros((3, 32, LANES))
    for ii in range(20):
        for a in range(20):
            q = ii * 20 + a
            ca[:20, q] = h[a]
            ci[:20, q] = h[ii]
            for k in range(3):
                folds[0, q, 32 * k + a] = 1
                folds[1, q, 32 * k + ii] = 1
        for k in range(3):
            wide[0, ii, 80 * k : 80 * k + 80] = np.repeat(h[ii], 4)
        for y in range(20):
            wide[1, ii, y * ZPAD : y * ZPAD + 20] = h[ii, y]
            wide[2, ii, y * ZPAD : y * ZPAD + 20] = h[ii]
    high = np.asarray(np.asarray(wide, np.float32).astype(jnp.bfloat16), np.float32)
    c["wide"] = np.concatenate([high, high, wide - high, np.zeros((3, 32, LANES))], axis=1)
    c["ca"], c["ci"], c["folds"] = ca, ci, folds
    po = np.zeros((160, 160))
    for xx in range(20):
        for r in range(8):
            po[(r // 2) * 40 + (r % 2) * 20 + xx, (r // 4) * 80 + xx * 4 + r % 4] = 1
    c["po"] = po
    return c


def _onehot(t):
    return jnp.asarray(t, BF16)


def _pair(t):
    t = np.asarray(t, np.float32)
    hi = t.astype(jnp.bfloat16)
    lo = (t - hi.astype(np.float32)).astype(jnp.bfloat16)
    return jnp.asarray(np.stack([hi, lo]))


def dot(a, b):
    return jnp.dot(a, b, preferred_element_type=F32)


def dot_nt(a, b):
    return lax.dot_general(a, b, (((1,), (1,)), ((), ())), preferred_element_type=F32)


def split2(v):
    hi = v.astype(BF16)
    return hi, (v - hi.astype(F32)).astype(BF16)


def split3(v):
    hi = v.astype(BF16)
    rest = v - hi.astype(F32)
    mid = rest.astype(BF16)
    return hi, mid, (rest - mid.astype(F32)).astype(BF16)


def dot3(a, b):
    ah, al = a
    bh, bl = b
    return dot(ah, bh) + (dot(al, bh) + dot(ah, bl))


def iota(shape, dim):
    return lax.broadcasted_iota(jnp.int32, shape, dim)


def placed(lanes):
    return (iota((LANES, LANES), 0) == lanes).astype(F32).astype(BF16)


def pack_kernel(leaf, td, ts, ct, pp, lanes, ra, hx, hy, wmsg, cmsg, rows):
    perm = placed(lanes[0:1, :])
    rows[...] = jnp.zeros_like(rows)
    for a in range(ORDER):
        rows[16 * a : 16 * a + 16, :100] = leaf[:, 100 * a : 100 * a + 100]
    w = jnp.zeros((40, LANES), F32)
    for part in split3(rows[...]):
        pieces = [dot(ra[o], part) for o in range(4)]
        w = w + dot(jnp.concatenate(pieces, axis=1).astype(BF16), perm)
    first = dot3((hx[0], hx[1]), split2(w))
    corner = dot3(split2(first), (hy[0], hy[1]))
    lane = iota((40, LANES), 1)
    row = iota((40, LANES), 0)
    for n in range(NODES1):
        mine = (row // EDGE) == n
        for e in range(DISP):
            w = jnp.where(mine & (lane == 480 + e), td[n, e].astype(F32), w)
            w = jnp.where(mine & (lane == 488 + e), ts[n, e].astype(F32), w)
    for k in range(8):
        wmsg[k] = w
    z = lax.axis_index("gz")
    lane2 = iota((24, 128), 1)
    row2 = iota((24, 128), 0)
    for n in range(NODES1):
        q = pp[0, z * NODES1 + n]
        corner = jnp.where((row2 == n) & (lane2 == 108), (q % 8).astype(F32), corner)
        for e in range(DISP):
            here = (row2 == n) & (lane2 == 100 + e)
            corner = jnp.where(here, ct[q // 8, e].astype(F32), corner)
    for k in range(32):
        cmsg[k] = corner


def prep_kernel(ob, ranks, ci, ca, folds, wide, a0, l1, l2, q0, q1, q2):
    level = pl.program_id(0)
    for e in range(DISP):
        for t in range(TERMS):
            k = e * TERMS + t
            keep = (t < ranks[level, e]).astype(F32)
            q0[24 * k : 24 * k + 24, :] = ob[0, e, t, 0:1, :] * keep * ci[...]
            q1[24 * k : 24 * k + 24, :] = ob[0, e, t, 1:2, :] * ca[...]
            q2[24 * k : 24 * k + 24, :] = ob[0, e, t, 2:3, :] * ca[...]

    def folded(q, fold, d):
        hi, lo = split2(q[...])
        both = dot(hi, fold) + dot(lo, fold)
        lane = iota(both.shape, 1) // 32
        rest = both - both.astype(BF16).astype(F32)
        return dot(jnp.where(lane == 1, rest, both).astype(BF16), wide[d])

    a0[0] = folded(q0, folds[0], 0)[:, :256]
    l1[0] = folded(q1, folds[1], 1)
    l2[0] = folded(q2, folds[1], 2)


def images(rank, sources, a0, l1, l2, acc, kh, kl, bd):
    @pl.when(pl.program_id(0) == 0)
    def _():
        acc[...] = jnp.zeros_like(acc)
        for t in range(TERMS):
            kh[t, 480:, :] = jnp.zeros((32, LANES), BF16)
            kl[t, 480:, :] = jnp.zeros((32, LANES), BF16)

    lane = iota((8, 256), 1)
    row = iota((8, 256), 0)
    same = jnp.where((lane % 4 == row % 4) & (lane < 240), 1.0, 0.0)
    for t in range(TERMS):
        for i in range(0, EDGE, 2):
            at = 24 * t + i
            value = jnp.where(row < 4, a0[0, at : at + 1, :], a0[0, at + 1 : at + 2, :]) * same
            rest = value - value.astype(BF16).astype(F32)
            bd[80 * t + 4 * i : 80 * t + 4 * i + 8, :] = jnp.where(lane < 160, value, rest)
    left = bd[...].astype(BF16)
    zero = jnp.zeros((16, LANES), BF16)
    mixed = []
    for source in sources:
        hi, lo = split2(source)
        mixed.append(dot(left, jnp.concatenate([hi, lo, hi, zero], axis=0)))

    def build(t):
        third = l2[0, 24 * t : 24 * t + 24, :]
        for y in range(0, EDGE, 2):
            one = l1[0, 24 * t + y : 24 * t + y + 1, :] * third
            two = l1[0, 24 * t + y + 1 : 24 * t + y + 2, :] * third
            hi, lo = split2(jnp.concatenate([one, two], axis=0))
            kh[t, ZPAD * y : ZPAD * y + 48, :] = hi
            kl[t, ZPAD * y : ZPAD * y + 48, :] = lo

    def term(t):
        rows = [m[80 * t : 80 * t + 80, :] for m in mixed]
        both = split2(rows[0] if len(rows) == 1 else jnp.concatenate(rows, axis=0))
        return dot3(both, (kh[t], kl[t]))

    build(0)
    build(1)
    acc[...] = acc[...] + (term(0) + term(1))
    for t in range(2, TERMS):

        @pl.when(rank > t)
        def _():
            build(t)
            acc[...] = acc[...] + term(t)


def coarse_kernel(corners, pp, ranks, a0, l1, l2, lanes, out, acc, kh, kl, bd, gs, sw, perm):
    e = pl.program_id(0)

    @pl.when(e == 0)
    def _():
        perm[...] = placed(lanes[0:1, :])
        parts = []
        for a in range(ORDER):
            pair = [corners[pl.ds(2 * a + n, 32, stride=24), :] for n in range(NODES1)]
            parts.append(jnp.concatenate(pair, axis=0))
        value = jnp.concatenate(parts, axis=1)
        sel = (iota((16, 128), 1) == iota((16, 128), 0) + 100).astype(F32).astype(BF16)
        info = dot_nt(sel, value[:, 0:128].astype(BF16))
        col = lax.axis_index("gx") * lax.axis_size("gy") + lax.axis_index("gy")
        r4 = iota((8, 64), 0) % 4
        want = jnp.where(r4 < C0, (col * C0 + r4), -1).astype(F32)
        octant = info[8:9, :]
        blocks = []
        for oyz in range(4):
            for d in range(DISP):
                hit = info[d : d + 1, :] == want
                for ox in range(2):
                    there = octant == float(4 * ox + oyz)
                    blocks.append(jnp.where(hit & there, 1.0, 0.0))
        pick = jnp.concatenate(blocks, axis=0).astype(BF16)
        hi, lo = split2(value)
        gs[...] = dot(pick, hi) + dot(pick, lo)

    half = iota((8, 128), 0) < 4
    for oyz in range(4):
        for ox in range(2):
            base = (oyz * DISP + e) * 16 + ox * 8
            for a in range(0, ORDER, 2):
                one = gs[pl.ds(base, 8), 128 * a : 128 * a + 128]
                two = gs[pl.ds(base, 8), 128 * a + 128 : 128 * a + 256]
                at = (ox * 10 + a) * 4
                sw[at : at + 8, 128 * oyz : 128 * oyz + 128] = jnp.where(half, one, two)
    hi, lo = split2(sw[...])
    source = dot(hi, perm[...]) + dot(lo, perm[...])
    images(ranks[0, e], [source], a0, l1, l2, acc, kh, kl, bd)

    @pl.when(e == DISP - 1)
    def _():
        back = placed(lanes[1:2, :])
        col = iota((ZPAD, 320), 1)
        code = ((col % 4) * 4 + col // 80) * EDGE + (col % 80) // 4
        row = iota((ZPAD, 320), 0)
        a = row % 12
        blocks = []
        for z in range(8):
            qs = [pp[0, NODES1 * z + n] for n in range(NODES1)]
            bases = [((q // 8) * 4 + q % 4) * EDGE + ((q % 8) // 4) * ORDER for q in qs]
            base = jnp.where(row < 12, bases[0], bases[1])
            blocks.append(jnp.where((a < ORDER) & (code == base + a), 1.0, 0.0))
        pick = jnp.concatenate(blocks, axis=0).astype(BF16)
        picked = jnp.zeros((192, 128), F32)
        for part in split3(acc[...]):
            moved = dot(part, back).astype(BF16)
            stacked = jnp.concatenate([moved[:, 128 * o : 128 * o + 128] for o in range(4)], axis=0)
            picked = picked + dot(pick, stacked)
        for z in range(8):
            out[z] = picked[ZPAD * z : ZPAD * z + ZPAD, :]


def middle_kernel(wall, ranks, a0, l1, l2, po, out, acc, kh, kl, bd, info, wsplit):
    e = pl.program_id(0)

    @pl.when(e == 0)
    def _():
        sel = (iota((16, 128), 1) == iota((16, 128), 0) + 96).astype(F32).astype(BF16)
        raw = dot_nt(sel, wall[:, 384:512].astype(BF16))
        device = raw[0:8, :]
        gy = jnp.floor(device * 0.125)
        gz = device - gy * 8.0
        z = lax.axis_index("gz").astype(F32)
        info[...] = jnp.where(gz == z, gy * 2.0 + raw[8:16, :], -1.0)
        hi, lo = split2(wall[...])
        wsplit[0] = hi
        wsplit[1] = lo

    lane = iota((160, 320), 1)
    row = iota((160, 320), 0)
    slot = (row // 80) * 4 + row % 4
    target = info[pl.ds(e, 1), :]
    hit = (lane % EDGE == (row % 80) // 4) & (target == slot.astype(F32))
    pick = jnp.where(hit, 1.0, 0.0).astype(BF16)
    source = dot(pick, wsplit[0]) + dot(pick, wsplit[1])
    images(ranks[1, e], [source[:80, :], source[80:, :]], a0, l1, l2, acc, kh, kl, bd)

    @pl.when(e == DISP - 1)
    def _():
        moved = jnp.zeros((160, LANES), F32)
        for part in split3(acc[...]):
            moved = moved + dot(po[...], part)
        for g in range(4):
            out[g] = moved[40 * g : 40 * g + 40, :]


def final_kernel(mid, coarse, lanes, ht, hyt, rt, out):
    back = placed(lanes[1:2, :])
    total = (mid[0] + mid[1]) + (mid[2] + mid[3])
    corner = coarse[0]
    for z in range(1, 8):
        corner = corner + coarse[z]
    up = dot3((ht[0], ht[1]), split2(corner))
    total = total + dot3(split2(up), (hyt[0], hyt[1]))
    rows = jnp.zeros((160, 128), F32)
    for part in split3(total):
        moved = dot(part, back).astype(BF16)
        stacked = jnp.concatenate([moved[:, 128 * o : 128 * o + 128] for o in range(4)], axis=0)
        rows = rows + dot(rt[...], stacked)
    for a in range(ORDER):
        out[:, 100 * a : 100 * a + 100] = rows[16 * a : 16 * a + 16, :100]


VM = pl.BlockSpec(memory_space=pltpu.MemorySpace.VMEM)
SM = pl.BlockSpec(memory_space=pltpu.MemorySpace.SMEM)
COST = pl.CostEstimate(flops=8_000_000_000, transcendentals=0, bytes_accessed=4_000_000)


def sds(*shape):
    return jax.ShapeDtypeStruct(shape, F32)


def _params():
    return pltpu.CompilerParams(vmem_limit_bytes=56 * 1024 * 1024)


def level_scratch(rows):
    return [
        pltpu.VMEM((rows, LANES), F32),
        pltpu.VMEM((TERMS, LANES, LANES), BF16),
        pltpu.VMEM((TERMS, LANES, LANES), BF16),
        pltpu.VMEM((TERMS * 80, 256), F32),
    ]


def const(shape):
    return pl.BlockSpec(shape, lambda *_: (0,) * len(shape))


def swap(value, axis):
    return lax.all_to_all(value, axis, split_axis=0, concat_axis=0, tiled=True)


def on_device(leaf, ob, ranks, td, ts, ct, pp):
    c = _tables()
    lanes = jnp.asarray(c["lanes"], jnp.int32)
    wmsg, cmsg = pl.pallas_call(
        pack_kernel,
        out_shape=(sds(8, 40, LANES), sds(32, 24, 128)),
        in_specs=[VM, SM, SM, SM, SM, VM, VM, VM, VM],
        out_specs=(VM, VM),
        scratch_shapes=[pltpu.VMEM((160, 128), F32)],
        compiler_params=_params(),
        name="pack",
    )(
        leaf,
        td.reshape(NODES1, DISP),
        ts,
        ct,
        pp,
        lanes,
        _onehot(c["ra"]),
        _pair(c["hx"]),
        _pair(c["hy"]),
    )
    corners = swap(cmsg, ("gx", "gy")).reshape(768, 128)
    rows = DISP * TERMS * 24
    mats = pl.pallas_call(
        prep_kernel,
        grid=(2,),
        out_shape=(sds(2, rows, 256), sds(2, rows, LANES), sds(2, rows, LANES)),
        in_specs=[
            pl.BlockSpec((1, DISP, TERMS, 3, 400), lambda l: (l, 0, 0, 0, 0)),
            SM,
            const((24, 400)),
            const((24, 400)),
            const((2, 400, 128)),
            const((3, 128, LANES)),
        ],
        out_specs=tuple(
            pl.BlockSpec((1, rows, n), lambda l: (l, 0, 0)) for n in (256, LANES, LANES)
        ),
        scratch_shapes=[pltpu.VMEM((rows, 400), F32)] * 3,
        compiler_params=_params(),
        cost_estimate=COST,
        name="prep",
    )(ob, ranks, jnp.asarray(c["ci"]), jnp.asarray(c["ca"]), _onehot(c["folds"]), _onehot(c["wide"]))
    wmsg, *mats = lax.optimization_barrier((wmsg, *mats))
    wall = swap(wmsg, "gz").reshape(320, LANES)

    def specs(level):
        def of(lanes):
            return pl.BlockSpec((1, 96, lanes), lambda e: (level, e, 0))

        return [of(256), of(LANES), of(LANES)]

    coarse = pl.pallas_call(
        coarse_kernel,
        grid=(DISP,),
        out_shape=sds(8, 24, 128),
        in_specs=[const((768, 128)), SM, SM, *specs(0), const((8, LANES))],
        out_specs=const((8, 24, 128)),
        scratch_shapes=[
            *level_scratch(80),
            pltpu.VMEM((448, 1280), F32),
            pltpu.VMEM((80, LANES), F32),
            pltpu.VMEM((LANES, LANES), BF16),
        ],
        compiler_params=_params(),
        cost_estimate=COST,
        name="coarse",
    )(corners, pp, ranks, *mats, lanes)
    middle = pl.pallas_call(
        middle_kernel,
        grid=(DISP,),
        out_shape=sds(4, 40, LANES),
        in_specs=[const((320, LANES)), SM, *specs(1), const((160, 160))],
        out_specs=const((4, 40, LANES)),
        scratch_shapes=[
            *level_scratch(160),
            pltpu.VMEM((8, 320), F32),
            pltpu.VMEM((2, 320, LANES), BF16),
        ],
        compiler_params=_params(),
        cost_estimate=COST,
        name="middle",
    )(wall, ranks, *mats, _onehot(c["po"]))
    coarse = swap(coarse, "gz")
    middle = swap(middle, "gy")
    return pl.pallas_call(
        final_kernel,
        out_shape=sds(16, 1000),
        in_specs=[VM] * 6,
        out_specs=VM,
        compiler_params=_params(),
        name="final",
    )(middle, coarse, lanes, _pair(c["ht"]), _pair(c["hyt"]), _onehot(c["rt"]))


def solution(mesh):
    in_specs = (
        P(("gx", "gy", "gz"), None),
        P(),
        P(),
        P(("gx", "gy", "gz"), None, None),
        P(("gx", "gy", "gz"), None),
        P(("gx", "gy"), None),
        P(("gx", "gy"), None),
    )
    out_specs = P(("gx", "gy", "gz"), None)
    return jax.shard_map(
        on_device, mesh=mesh, in_specs=in_specs, out_specs=out_specs, check_vma=False
    )
```

time: 106 us -> 83.8 us (0.79)
  blocking collectives: 27.9 us -> 11.7 us
  Pallas kernels: 56.9 us -> 44.1 us
  starting transfers between devices: 15.8 us -> 20.6 us
  waiting for transfers between devices: 0.01 us -> 4.06 us
  local copies, waits for them, and re-layouts: 4.5 us -> 1.94 us
    all_to_all x2 -> x1, blocking collectives: 27.9 us -> 11.7 us  [swap(): return lax.all_to_all(value, axis, split_axis=0, concat_axis=0, tiled=True)]
    pallas_call x1, Pallas kernels: 21.6 us -> 15.5 us  [on_device(): pl.pallas_call(coarse_kernel, grid=(DISP,), out_shape=sds(8, 24, 128), in...]
    pallas_call x1, Pallas kernels: 20.2 us -> 14.7 us  [on_device(): pl.pallas_call(middle_kernel, grid=(DISP,), out_shape=sds(4, 40, LANES),...]
    all_to_all x2 -> x3, starting transfers between devices: 15.8 us -> 20.6 us  [swap(): return lax.all_to_all(value, axis, split_axis=0, concat_axis=0, tiled=True)]
    all_to_all x2 -> x3, waiting for transfers between devices: 0.01 us -> 4.06 us  [swap(): return lax.all_to_all(value, axis, split_axis=0, concat_axis=0, tiled=True)]
    broadcast_in_dim x2 -> x0, local copies, waits for them, and re-layouts: 2.59 us -> none  [gather_rows(): copies = jnp.broadcast_to(value, (lax.axis_size(axis), *value.shape))]
    pallas_call x2, Pallas kernels: 12 us -> 11 us  [the longest x1 7.93 us: on_device(): pl.pallas_call(prep_kernel, grid=(2,), out_shape=(sds(2, rows, 256), sds(...]
  transfers between devices with their start and end apart: 2 -> 3, of which waited for: 0 -> 2; matrix products, arithmetic and copies ran while one was open for 2% -> 2% of each run, Pallas kernels for 48% -> 46%
where the time goes in v1:
time: 83.8 us; the launch traced here: 82.4 us
  Pallas kernels  44.1 us (53%)
  starting transfers between devices  20.6 us (25%)
  blocking collectives  11.7 us (14%)
  waiting for transfers between devices  4.06 us (5%)
  local copies, waits for them, and re-layouts  1.94 us (2%)
    all_to_all x3, starting transfers between devices, swap(): return lax.all_to_all(value, axis, split_axis=0, concat_axis=0, tiled=True)  20.6 us
    pallas_call x1, Pallas kernels, on_device(): pl.pallas_call(coarse_kernel, grid=(DISP,), out_shape=sds(8, 24, 128), in...  15.5 us
    pallas_call x1, Pallas kernels, on_device(): pl.pallas_call(middle_kernel, grid=(DISP,), out_shape=sds(4, 40, LANES),...  14.7 us
    all_to_all x1, blocking collectives, swap(): return lax.all_to_all(value, axis, split_axis=0, concat_axis=0, tiled=True)  11.7 us
    pallas_call x1, Pallas kernels, on_device(): pl.pallas_call(prep_kernel, grid=(2,), out_shape=(sds(2, rows, 256), sds(...  7.93 us
    all_to_all x3, waiting for transfers between devices, swap(): return lax.all_to_all(value, axis, split_axis=0, concat_axis=0, tiled=True)  4.06 us
    pallas_call x1, Pallas kernels, on_device(): pl.pallas_call(pack_kernel, out_shape=(sds(8, 40, LANES), sds(32, 24, 128...  3.04 us
    pallas_call x1, Pallas kernels, on_device(): pl.pallas_call(final_kernel, out_shape=sds(16, 1000), in_specs=[VM] * 6,...  2.9 us
  transfers between devices with their start and end apart: 3, of which 2 were waited for; matrix products, arithmetic and copies ran while one was open for 2% of the time, Pallas kernels for 46%

profile of v1, /device:TPU:32, one launch (start us, length us, event | category | flops | bytes accessed | tf_op | source)
XLA Modules:
  0.0 82.4 jit_solution(14836662161018243489)
XLA Ops:
  0.0 3.0 %pack.1 = (f32[8,40,512]{2,1,0:T(8,128)}, f32[32,24,128]{2,1,0:T(8,128)}) custom-call(f32[16,1000]{1,0:T(8,128)} %leaf.1, s32[2,7]{1,0:T(2,128)} %bitcast.5, s32[2,7]{1,0:T(2,128)} %ts.1, s32[3,7]{1,0:T(4,128)} %ct.1, s32[1,16]{1,0:T(1,128)} %pp.3, s32[8,512]{1,0:T(8,128)} %constant.24.clone.lanes, bf16[4,40,160]{2,1,0:T(8,128)(2,1)} %constant.25.clone.ra, ...), custom_call_target="tpu_custom_call" | custom-call | tf_op jit(solution)/shard_map/pack/pallas_call | solution.py:388
  3.0 7.3 %all-to-all-start.2 = ((f32[32,24,128]{2,1,0:T(8,128)}), f32[32,24,128]{2,1,0:T(8,128)S(1)}, u32[]{:S(2)}, u32[]{:S(2)}) async-start(f32[32,24,128]{2,1,0:T(8,128)} %get-tuple-element.22), calls=%async_computation.2 | async-start | bytes 786432 | tf_op jit(solution)/shard_map/all_to_all | solution.py:382
  10.4 1.9 %copy.20.ob = f32[2,7,4,3,400]{4,3,2,1,0:T(4,128)} copy(f32[2,7,4,3,400]{4,2,3,1,0:T(4,128)} %param.20) | data formatting | bytes 537600 | tf_op args[1]
  12.3 7.9 %prep.1 = (f32[2,672,256]{2,1,0:T(8,128)}, f32[2,672,512]{2,1,0:T(8,128)}, f32[2,672,512]{2,1,0:T(8,128)}) custom-call(f32[2,7,4,3,400]{4,3,2,1,0:T(4,128)} %copy.20.ob, s32[2,7]{1,0:T(2,128)} %ranks.5, f32[24,400]{1,0:T(8,128)} %constant.28.clone.ci, f32[24,400]{1,0:T(8,128)} %constant.29.clone.ca, bf16[2,400,128]{2,1,0:T(8,128)(2,1)} %constant.30.clone.folds, ...), custom_call_target="tpu_custom_call" | custom-call | flops 8000000000 | bytes 4000000 | tf_op jit(solution)/shard_map/prep/pallas_call | solution.py:409
  20.2 0.5 all-to-all-done.2
  20.7 0.0 copy-start.1
  20.7 8.6 %all-to-all-start = ((f32[8,40,512]{2,1,0:T(8,128)}), f32[8,40,512]{2,1,0:T(8,128)S(1)}, u32[]{:S(2)}, u32[]{:S(2)}) async-start(f32[8,40,512]{2,1,0:T(8,128)} %get-tuple-element.18), calls=%async_computation | async-start | bytes 1310720 | tf_op jit(solution)/shard_map/all_to_all | solution.py:382
  29.3 0.0 copy-done.1
  29.3 15.5 %coarse.1 = f32[8,24,128]{2,1,0:T(8,128)} custom-call(f32[768,128]{1,0:T(8,128)} %bitcast.4, s32[1,16]{1,0:T(1,128)} %pp.3, s32[2,7]{1,0:T(2,128)} %ranks.5, f32[2,672,256]{2,1,0:T(8,128)} %get-tuple-element.19.a0, f32[2,672,512]{2,1,0:T(8,128)} %get-tuple-element.20.l1, f32[2,672,512]{2,1,0:T(8,128)} %get-tuple-element.21.l2, s32[8,512]{1,0:T(8,128)} %constant.24.clone.lanes), custom_call_target="tpu_custom_call" | custom-call | flops 8000000000 | bytes 4000000 | tf_op jit(solution)/shard_map/coarse/pallas_call | solution.py:438
  44.8 3.6 %all-to-all-done = f32[8,40,512]{2,1,0:T(8,128)S(1)} async-done(((f32[8,40,512]{2,1,0:T(8,128)}), f32[8,40,512]{2,1,0:T(8,128)S(1)}, u32[]{:S(2)}, u32[]{:S(2)}) %all-to-all-start) | async-done | bytes 655392 | tf_op jit(solution)/shard_map/all_to_all | solution.py:382
  48.4 0.0 copy-start
  48.4 4.7 %all-to-all-start.3 = ((f32[8,24,128]{2,1,0:T(8,128)}), f32[8,24,128]{2,1,0:T(8,128)S(1)}, u32[]{:S(2)}, u32[]{:S(2)}) async-start(f32[8,24,128]{2,1,0:T(8,128)} %coarse.1), calls=%async_computation.3 | async-start | bytes 196608 | tf_op jit(solution)/shard_map/all_to_all | solution.py:382
  53.1 0.0 copy-done
  53.1 14.7 %middle.1 = f32[4,40,512]{2,1,0:T(8,128)} custom-call(f32[320,512]{1,0:T(8,128)} %bitcast.3, s32[2,7]{1,0:T(2,128)} %ranks.5, f32[2,672,256]{2,1,0:T(8,128)} %get-tuple-element.19.a0, f32[2,672,512]{2,1,0:T(8,128)} %get-tuple-element.20.l1, f32[2,672,512]{2,1,0:T(8,128)} %get-tuple-element.21.l2, bf16[160,160]{1,0:T(8,128)(2,1)} %constant.32.clone.po), custom_call_target="tpu_custom_call" | custom-call | flops 8000000000 | bytes 4000000 | tf_op jit(solution)/shard_map/middle/pallas_call | solution.py:454
  67.8 0.0 all-to-all-done.3.coarse
  67.8 0.0 copy-start.2
  67.8 11.7 %all_to_all.20.mid = f32[4,40,512]{2,1,0:T(8,128)} all-to-all(f32[4,40,512]{2,1,0:T(8,128)} %middle.1), channel_id=1, replica_groups=mesh['gx'=8,'gy'=4,'gz'=8] {'gy'}, dimensions={0} | all-to-all | bytes 655360 | tf_op jit(solution)/shard_map/all_to_all | solution.py:382
  79.5 0.0 copy-done.2
  79.5 2.9 %final.1 = f32[16,1000]{1,0:T(8,128)} custom-call(f32[4,40,512]{2,1,0:T(8,128)} %all_to_all.20.mid, f32[8,24,128]{2,1,0:T(8,128)} %copy-done.2, s32[8,512]{1,0:T(8,128)} %constant.24.clone.lanes, bf16[2,40,24]{2,1,0:T(8,128)(2,1)} %constant.33.clone.ht, bf16[2,128,512]{2,1,0:T(8,128)(2,1)} %constant.34.clone.hyt, bf16[160,160]{1,0:T(8,128)(2,1)} %constant.35.clone.rt), custom_call_target="tpu_custom_call" | custom-call | tf_op jit(solution)/shard_map/final/pallas_call | solution.py:471
Async XLA Ops:
  3.0 17.6 %all-to-all-start.2 = ((f32[32,24,128]{2,1,0:T(8,128)}), f32[32,24,128]{2,1,0:T(8,128)S(1)}, u32[]{:S(2)}, u32[]{:S(2)}) async-start(f32[32,24,128]{2,1,0:T(8,128)} %get-tuple-element.22), calls=%async_computation.2 | async-start | bytes 786432 | tf_op jit(solution)/shard_map/all_to_all | solution.py:382
  20.7 8.6 %copy-start.1 = (f32[32,24,128]{2,1,0:T(8,128)}, f32[32,24,128]{2,1,0:T(8,128)S(1)}, u32[]{:S(2)}) copy-start(f32[32,24,128]{2,1,0:T(8,128)S(1)} %all-to-all-done.2) | copy-start | bytes 1179652
  20.7 27.7 %all-to-all-start = ((f32[8,40,512]{2,1,0:T(8,128)}), f32[8,40,512]{2,1,0:T(8,128)S(1)}, u32[]{:S(2)}, u32[]{:S(2)}) async-start(f32[8,40,512]{2,1,0:T(8,128)} %get-tuple-element.18), calls=%async_computation | async-start | bytes 1310720 | tf_op jit(solution)/shard_map/all_to_all | solution.py:382
  48.4 4.7 %copy-start = (f32[8,40,512]{2,1,0:T(8,128)}, f32[8,40,512]{2,1,0:T(8,128)S(1)}, u32[]{:S(2)}) copy-start(f32[8,40,512]{2,1,0:T(8,128)S(1)} %all-to-all-done) | copy-start | bytes 1966084
  48.4 19.4 %all-to-all-start.3 = ((f32[8,24,128]{2,1,0:T(8,128)}), f32[8,24,128]{2,1,0:T(8,128)S(1)}, u32[]{:S(2)}, u32[]{:S(2)}) async-start(f32[8,24,128]{2,1,0:T(8,128)} %coarse.1), calls=%async_computation.3 | async-start | bytes 196608 | tf_op jit(solution)/shard_map/all_to_all | solution.py:382
  67.8 11.7 %copy-start.2 = (f32[8,24,128]{2,1,0:T(8,128)}, f32[8,24,128]{2,1,0:T(8,128)S(1)}, u32[]{:S(2)}) copy-start(f32[8,24,128]{2,1,0:T(8,128)S(1)} %all-to-all-done.3.coarse) | copy-start | bytes 294916
